TPU v7x, 256 devices: a whole 4x4x8 slice. The times are simulated.
256 devices in a mesh: row: 16 (over x, y), col: 16 (over z, core).
Axes of the slice: x: 4, y: 4, z: 8, core: 2. Of those that a mesh axis runs over, the one named last changes fastest.
Arguments:
- values: bfloat16 [8192, 8192], P('row', 'col'), may hold values from 0.0001296997 to 0.12988281
- tile_mask: int32 [64, 64], P('row', 'col'), may hold values 0 or 1
- keep_mask: int32 [64, 64], P('row', 'col'), may hold values 0 or 1
- thr_index: int32 [8192], P('col'), may hold values from 0 to 9
Outputs:
- expanded: bfloat16 [8192, 8192], P('row', 'col')
All inputs are finite; a program needn't handle non-finite values. No bound on the sum of `tile_mask` or of `keep_mask` on one device may be relied on, other than what follows from the above.
Results may differ from a plain program's by a relative error of at most 0.0004.
Values may be sent and summed in bfloat16 or wider, within the bound.
A program may use at most 64 MiB of HBM per device.

v0:
```python
import jax
import jax.numpy as jnp
from jax import lax
from jax.sharding import Mesh
from jax.sharding import PartitionSpec as P

TB = 128
ROW = ("row_0", "row_1")


def over_axes(x, axes):
    for axis in axes:
        x = lax.psum(x, axis)
    return x


def on_device(values, tile_mask, keep_mask, thr_index):
    row_count, col_count = values.shape
    row_tiles = row_count // TB
    col_tiles = col_count // TB
    matrix = (
        values.reshape(row_tiles, TB, col_tiles, TB)
        * tile_mask[:, None, :, None].astype(jnp.bfloat16)
    ).reshape(row_count, col_count)
    kept_cells = jnp.broadcast_to(
        keep_mask[:, None, :, None].astype(jnp.float32), (row_tiles, TB, col_tiles, TB)
    ).reshape(row_count, col_count)
    order_all = row_count * lax.axis_size(ROW)
    thresholds = 0.125 * thr_index.astype(jnp.float32)
    col_panel = lax.all_gather(matrix, ROW, axis=0, tiled=True)
    product = jnp.dot(
        lax.all_gather(matrix, "col", axis=1, tiled=True),
        col_panel,
        preferred_element_type=jnp.float32,
    )
    outputs = []
    for phase_idx in range(col_tiles):
        lo_col = phase_idx * TB
        part_prod = product[:, lo_col : lo_col + TB]
        col_means = over_axes(jnp.sum(part_prod, axis=0), ROW) / order_all
        pruned = (
            jnp.maximum(part_prod - thresholds[lo_col : lo_col + TB] * col_means, 0.0)
            * kept_cells[:, lo_col : lo_col + TB]
        )
        col_totals = over_axes(jnp.sum(pruned, axis=0), ROW) / order_all
        outputs.append(pruned / jnp.maximum(col_totals, 0.1))
    result = jnp.concatenate(outputs, axis=1)
    return result.astype(jnp.bfloat16)


def solution(mesh):
    finer = Mesh(mesh.devices.reshape(4, 4, mesh.shape["col"]), ("row_0", "row_1", "col"))
    placed = (P(ROW, "col"), P(ROW, "col"), P(ROW, "col"), P("col"))
    return jax.shard_map(
        on_device, mesh=finer, in_specs=placed, out_specs=P(ROW, "col"), check_vma=False
    )
```

profile of v0, /device:TPU:2, one launch (start us, length us, event | category | flops | bytes accessed | tf_op | source)
XLA Modules:
  0.0 198.9 jit_solution(1561034129201004434)
XLA Ops:
  6.5 0.0 all-gather.3.cloned.1.call-start
  6.5 0.7 convert_element_type.12
  7.2 0.2 mul.41
  7.4 1.9 bitcast_multiply_fusion
  9.3 0.0 all-gather.3.cloned.1.call-update
  9.4 0.0 all-gather.5.cloned.1.call-start
  9.4 0.7 all-gather.5.cloned.1.call-update
  10.1 0.7 convert_element_type.14
  10.8 0.2 broadcast_in_dim.2
  11.0 0.1 copy.9
  11.1 0.7 convert_multiply_fusion
  11.8 56.5 %all-gather.3.cloned.1.call-done = bf16[512,8192]{1,0:T(8,128)(2,1)} async-done(((bf16[512,512]{1,0:T(8,128)(2,1)}), bf16[512,8192]{1,0:T(8,128)(2,1)}) %all-gather.3.cloned.1.call-update) | async-done | bytes 8388624 | tf_op jit(solution)/shard_map/all_gather | solution.py:32
  68.3 76.8 %all-gather.5.cloned.1.call-done = bf16[8192,512]{1,0:T(8,128)(2,1)} async-done(((bf16[512,512]{1,0:T(8,128)(2,1)}), bf16[8192,512]{1,0:T(8,128)(2,1)}) %all-gather.5.cloned.1.call-update) | async-done | bytes 8388624 | tf_op jit(solution)/shard_map/all_gather | solution.py:30
  145.1 9.4 %fusion.4 = f32[512,512]{1,0:T(8,128)S(1)} fusion(bf16[512,8192]{1,0:T(8,128)(2,1)} %all-gather.3.cloned.1.call-done, bf16[8192,512]{1,0:T(8,128)(2,1)} %all-gather.5.cloned.1.call-done), kind=kOutput, calls=%fused_computation.28 | convolution fusion | flops 4294967296 | bytes 17825792 | tf_op jit(solution)/shard_map/dot_general | solution.py:31
  154.6 0.1 slice_reduce_fusion.3
  154.7 8.6 %all-reduce.3 = (f32[128]{0:T(128)S(1)}, f32[128]{0:T(128)S(1)}, f32[128]{0:T(128)S(1)}, f32[128]{0:T(128)S(1)}) all-reduce(f32[128]{0:T(128)S(1)} %get-tuple-element.9, f32[128]{0:T(128)S(1)} %get-tuple-element.10, f32[128]{0:T(128)S(1)} %get-tuple-element.11, ...), channel_id=1, replica_groups=mesh['row_0'=4,'row_1'=4,'col'=16] {'row_0'}, use_global_device_ids=true, to_apply=%region_1.0 | all-reduce | flops 512 | bytes 4096 | tf_op jit(solution)/shard_map/psum | solution.py:13
  163.3 10.1 %all-reduce.1 = (f32[128]{0:T(128)S(1)}, f32[128]{0:T(128)S(1)}, f32[128]{0:T(128)S(1)}, f32[128]{0:T(128)S(1)}) all-reduce(f32[128]{0:T(128)S(1)} %get-tuple-element.25, f32[128]{0:T(128)S(1)} %get-tuple-element.26, f32[128]{0:T(128)S(1)} %get-tuple-element.27, ...), channel_id=1, replica_groups=mesh['row_0'=4,'row_1'=4,'col'=16] {'row_1'}, use_global_device_ids=true, to_apply=%region_2.0 | all-reduce | flops 512 | bytes 4096 | tf_op jit(solution)/shard_map/psum | solution.py:13
  173.4 0.2 fusion
  173.5 8.6 %all-reduce.2 = (f32[128]{0:T(128)S(1)}, f32[128]{0:T(128)S(1)}, f32[128]{0:T(128)S(1)}, f32[128]{0:T(128)S(1)}) all-reduce(f32[128]{0:T(128)S(1)} %get-tuple-element.6, f32[128]{0:T(128)S(1)} %get-tuple-element.7, f32[128]{0:T(128)S(1)} %get-tuple-element.8, ...), channel_id=1, replica_groups=mesh['row_0'=4,'row_1'=4,'col'=16] {'row_0'}, use_global_device_ids=true, to_apply=%region_22.0 | all-reduce | flops 512 | bytes 4096 | tf_op jit(solution)/shard_map/psum | solution.py:13
  182.1 8.9 %all-reduce = (f32[128]{0:T(128)S(1)}, f32[128]{0:T(128)S(1)}, f32[128]{0:T(128)S(1)}, f32[128]{0:T(128)S(1)}) all-reduce(f32[128]{0:T(128)S(1)} %get-tuple-element.21, f32[128]{0:T(128)S(1)} %get-tuple-element.22, f32[128]{0:T(128)S(1)} %get-tuple-element.23, ...), channel_id=1, replica_groups=mesh['row_0'=4,'row_1'=4,'col'=16] {'row_1'}, use_global_device_ids=true, to_apply=%region_23.0 | all-reduce | flops 512 | bytes 4096 | tf_op jit(solution)/shard_map/psum | solution.py:13
  191.1 0.2 divide_convert_fusion.3
  191.2 0.9 pad_maximum_fusion
  (3 shorter events, 0.0 us)
Async XLA Ops:
  6.5 61.8 %all-gather.3.cloned.1.call-start = ((), (), s32[]{:S(2)}) async-start(), calls=%async_computation | async-start | bytes 8912896 | tf_op jit(solution)/shard_map/all_gather | solution.py:32
  9.4 135.8 %all-gather.5.cloned.1.call-start = ((), (), s32[]{:S(2)}) async-start(), calls=%async_computation.1 | async-start | bytes 8912896 | tf_op jit(solution)/shard_map/all_gather | solution.py:30
Sparse Core Ops, SparseCore 0:
  9.5 58.7 all-gather.2
  70.7 74.3 all-gather.4
where the time goes:
time: 199 us
  waiting for transfers between devices  134 us (67%)
  blocking collectives  36.2 us (18%)
  between operations  13.4 us (7%)
  matrix products  9.44 us (5%)
  other arithmetic  5.27 us (3%)
    all_gather x1, waiting for transfers between devices, on_device(): col_panel = lax.all_gather(matrix, ROW, axis=0, tiled=True)  76.8 us
    all_gather x1, waiting for transfers between devices, on_device(): lax.all_gather(matrix, 'col', axis=1, tiled=True)  56.5 us
    psum x4, blocking collectives, over_axes(): x = lax.psum(x, axis)  36.2 us
    dot_general x1, matrix products, on_device(): jnp.dot(lax.all_gather(matrix, 'col', axis=1, tiled=True), col_panel, pre...  9.44 us
  transfers between devices with their start and end apart: 2, of which 2 were waited for; matrix products, arithmetic and copies ran while one was open for 1% of the time, Pallas kernels for 0%

commit v1 on v0

--- a/solution.py
+++ b/solution.py
@@ -6,6 +6,19 @@
 
 TB = 128
 ROW = ("row_0", "row_1")
+
+
+def collect(x, axis, dim):
+    ways = lax.axis_size(axis)
+    up = [(d, (d + 1) % ways) for d in range(ways)]
+    down = [(d, (d - 1) % ways) for d in range(ways)]
+    earlier, later = ([x], [x])
+    for _ in range(ways // 2):
+        earlier.append(lax.ppermute(earlier[-1], axis, up))
+    for _ in range((ways - 1) // 2):
+        later.append(lax.ppermute(later[-1], axis, down))
+    line = jnp.concatenate([*earlier[::-1], *later[1:]], axis=dim)
+    return jnp.roll(line, (lax.axis_index(axis) - ways // 2) * x.shape[dim], axis=dim)
 
 
 def over_axes(x, axes):
@@ -28,11 +41,7 @@
     order_all = row_count * lax.axis_size(ROW)
     thresholds = 0.125 * thr_index.astype(jnp.float32)
     col_panel = lax.all_gather(matrix, ROW, axis=0, tiled=True)
-    product = jnp.dot(
-        lax.all_gather(matrix, "col", axis=1, tiled=True),
-        col_panel,
-        preferred_element_type=jnp.float32,
-    )
+    product = jnp.dot(collect(matrix, "col", 1), col_panel, preferred_element_type=jnp.float32)
     outputs = []
     for phase_idx in range(col_tiles):
         lo_col = phase_idx * TB

time: 199 us -> 191 us (0.960)
  waiting for transfers between devices: 134 us -> 55 us
  local copies, waits for them, and re-layouts: 0.48 us -> 46 us
  starting transfers between devices: 0.04 us -> 23.1 us
    all_gather x1, waiting for transfers between devices: 76.8 us -> 0.01 us  [on_device(): col_panel = lax.all_gather(matrix, ROW, axis=0, tiled=True)]
    all_gather x1 -> x0, waiting for transfers between devices: 56.5 us -> none  [on_device(): lax.all_gather(matrix, 'col', axis=1, tiled=True)]
    ppermute x0 -> x15, waiting for transfers between devices: none -> 55 us  [the longest x8 49.2 us: collect(): earlier.append(lax.ppermute(earlier[-1], axis, up))]
    unnamed x1 -> x62, local copies, waits for them, and re-layouts: 0.07 us -> 44.7 us
    ppermute x0 -> x15, starting transfers between devices: none -> 23.1 us  [the longest x7 23 us: collect(): later.append(lax.ppermute(later[-1], axis, down))]
  transfers between devices with their start and end apart: 2 -> 16, of which waited for: 2 -> 14; matrix products, arithmetic and copies ran while one was open for 1% -> 24% of each run, Pallas kernels for 0% -> 0%
where the time goes in v1:
time: 191 us; the launch traced here: 190 us
  waiting for transfers between devices  55 us (29%)
  local copies, waits for them, and re-layouts  46 us (24%)
  blocking collectives  37.2 us (19%)
  starting transfers between devices  23.1 us (12%)
  between operations  13.6 us (7%)
  matrix products  9.33 us (5%)
  other arithmetic  5.41 us (3%)
    ppermute x8, waiting for transfers between devices, collect(): earlier.append(lax.ppermute(earlier[-1], axis, up))  49.2 us
    unnamed x62, local copies, waits for them, and re-layouts  44.7 us
    psum x4, blocking collectives, over_axes(): x = lax.psum(x, axis)  37.2 us
    ppermute x7, starting transfers between devices, collect(): later.append(lax.ppermute(later[-1], axis, down))  23 us
    dot_general x1, matrix products, on_device(): jnp.dot(collect(matrix, 'col', 1), col_panel, preferred_element_type=jnp....  9.33 us
    ppermute x7, waiting for transfers between devices, collect(): later.append(lax.ppermute(later[-1], axis, down))  5.79 us
  transfers between devices with their start and end apart: 16, of which 14 were waited for; matrix products, arithmetic and copies ran while one was open for 24% of the time, Pallas kernels for 0%

profile of v1, /device:TPU:2, one launch (start us, length us, event | category | flops | bytes accessed | tf_op | source)
XLA Modules:
  0.0 189.6 jit_solution(2530109634139548422)
XLA Ops:
  7.4 1.9 %bitcast_multiply_fusion = bf16[512,512]{1,0:T(8,128)(2,1)} fusion(bf16[512,512]{1,0:T(8,128)(2,1)} %param.4, bf16[64,8,4,128]{3,2,1,0:T(4,128)(2,1)S(1)} %bitcast.13), kind=kLoop, calls=%fused_computation.3 | loop fusion | flops 262144 | bytes 1572864 | tf_op jit(solution)/shard_map/mul | solution.py:35
  9.4 12.4 %collective-permute-done = bf16[512,512]{1,0:T(8,128)(2,1)S(1)} collective-permute-done((bf16[512,512]{1,0:T(8,128)(2,1)}, bf16[512,512]{1,0:T(8,128)(2,1)S(1)}, u32[]{:S(2)}, u32[]{:S(2)}) %collective-permute-start) | collective-permute-done | bytes 524320 | tf_op jit(solution)/shard_map/ppermute | solution.py:17
  21.8 3.0 %collective-permute-start.8 = (bf16[512,512]{1,0:T(8,128)(2,1)}, bf16[512,512]{1,0:T(8,128)(2,1)S(1)}, u32[]{:S(2)}, u32[]{:S(2)}) collective-permute-start(bf16[512,512]{1,0:T(8,128)(2,1)} %bitcast_multiply_fusion), channel_id=1, source_target_pairs={{0,15},{1,0},{2,1},{3,2},{4,3},{5,4},{6,5},{7,6},{8,7},{9,8},{10,9... | collective-permute-start | bytes 1572872 | tf_op jit(solution)/shard_map/ppermute | solution.py:19
  24.7 6.9 %collective-permute-done.1 = bf16[512,512]{1,0:T(8,128)(2,1)S(1)} collective-permute-done((bf16[512,512]{1,0:T(8,128)(2,1)S(1)}, bf16[512,512]{1,0:T(8,128)(2,1)S(1)}, u32[]{:S(2)}, u32[]{:S(2)}) %collective-permute-start.1) | collective-permute-done | bytes 524320 | tf_op jit(solution)/shard_map/ppermute | solution.py:17
  31.8 3.4 %collective-permute-start.9 = (bf16[512,512]{1,0:T(8,128)(2,1)S(1)}, bf16[512,512]{1,0:T(8,128)(2,1)S(1)}, u32[]{:S(2)}, u32[]{:S(2)}) collective-permute-start(bf16[512,512]{1,0:T(8,128)(2,1)S(1)} %collective-permute-done.8), channel_id=1, source_target_pairs={{0,15},{1,0},{2,1},{3,2},{4,3},{5,4},{6,5},{7,6},{8,7},{9,8},{10,9... | collective-permute-start | bytes 1572872 | tf_op jit(solution)/shard_map/ppermute | solution.py:19
  35.2 6.2 %collective-permute-done.2 = bf16[512,512]{1,0:T(8,128)(2,1)S(1)} collective-permute-done((bf16[512,512]{1,0:T(8,128)(2,1)S(1)}, bf16[512,512]{1,0:T(8,128)(2,1)S(1)}, u32[]{:S(2)}, u32[]{:S(2)}) %collective-permute-start.2) | collective-permute-done | bytes 524320 | tf_op jit(solution)/shard_map/ppermute | solution.py:17
  41.9 3.1 %collective-permute-start.10 = (bf16[512,512]{1,0:T(8,128)(2,1)S(1)}, bf16[512,512]{1,0:T(8,128)(2,1)S(1)}, u32[]{:S(2)}, u32[]{:S(2)}) collective-permute-start(bf16[512,512]{1,0:T(8,128)(2,1)S(1)} %collective-permute-done.9), channel_id=1, source_target_pairs={{0,15},{1,0},{2,1},{3,2},{4,3},{5,4},{6,5},{7,6},{8,7},{9,8},{10,9... | collective-permute-start | bytes 1572872 | tf_op jit(solution)/shard_map/ppermute | solution.py:19
  45.0 6.2 %collective-permute-done.3 = bf16[512,512]{1,0:T(8,128)(2,1)S(1)} collective-permute-done((bf16[512,512]{1,0:T(8,128)(2,1)S(1)}, bf16[512,512]{1,0:T(8,128)(2,1)S(1)}, u32[]{:S(2)}, u32[]{:S(2)}) %collective-permute-start.3) | collective-permute-done | bytes 524320 | tf_op jit(solution)/shard_map/ppermute | solution.py:17
  52.5 3.1 %collective-permute-start.11 = (bf16[512,512]{1,0:T(8,128)(2,1)S(1)}, bf16[512,512]{1,0:T(8,128)(2,1)S(1)}, u32[]{:S(2)}, u32[]{:S(2)}) collective-permute-start(bf16[512,512]{1,0:T(8,128)(2,1)S(1)} %collective-permute-done.10), channel_id=1, source_target_pairs={{0,15},{1,0},{2,1},{3,2},{4,3},{5,4},{6,5},{7,6},{8,7},{9,8},{10,9... | collective-permute-start | bytes 1572872 | tf_op jit(solution)/shard_map/ppermute | solution.py:19
  55.6 5.5 %collective-permute-done.4 = bf16[512,512]{1,0:T(8,128)(2,1)S(1)} collective-permute-done((bf16[512,512]{1,0:T(8,128)(2,1)S(1)}, bf16[512,512]{1,0:T(8,128)(2,1)S(1)}, u32[]{:S(2)}, u32[]{:S(2)}) %collective-permute-start.4) | collective-permute-done | bytes 524320 | tf_op jit(solution)/shard_map/ppermute | solution.py:17
  61.1 1.2 collective-permute-done.11
  63.1 3.5 %collective-permute-start.12 = (bf16[512,512]{1,0:T(8,128)(2,1)S(1)}, bf16[512,512]{1,0:T(8,128)(2,1)}, u32[]{:S(2)}, u32[]{:S(2)}) collective-permute-start(bf16[512,512]{1,0:T(8,128)(2,1)S(1)} %collective-permute-done.11), channel_id=1, source_target_pairs={{0,15},{1,0},{2,1},{3,2},{4,3},{5,4},{6,5},{7,6},{8,7},{9,8},{10,9... | collective-permute-start | bytes 1572872 | tf_op jit(solution)/shard_map/ppermute | solution.py:19
  66.6 4.3 %collective-permute-done.5 = bf16[512,512]{1,0:T(8,128)(2,1)S(1)} collective-permute-done((bf16[512,512]{1,0:T(8,128)(2,1)S(1)}, bf16[512,512]{1,0:T(8,128)(2,1)S(1)}, u32[]{:S(2)}, u32[]{:S(2)}) %collective-permute-start.5) | collective-permute-done | bytes 524320 | tf_op jit(solution)/shard_map/ppermute | solution.py:17
  70.9 2.4 %collective-permute-done.12 = bf16[512,512]{1,0:T(8,128)(2,1)} collective-permute-done((bf16[512,512]{1,0:T(8,128)(2,1)S(1)}, bf16[512,512]{1,0:T(8,128)(2,1)}, u32[]{:S(2)}, u32[]{:S(2)}) %collective-permute-start.12) | collective-permute-done | bytes 524320 | tf_op jit(solution)/shard_map/ppermute | solution.py:19
  73.3 3.5 %collective-permute-start.13 = (bf16[512,512]{1,0:T(8,128)(2,1)}, bf16[512,512]{1,0:T(8,128)(2,1)}, u32[]{:S(2)}, u32[]{:S(2)}) collective-permute-start(bf16[512,512]{1,0:T(8,128)(2,1)} %collective-permute-done.12), channel_id=1, source_target_pairs={{0,15},{1,0},{2,1},{3,2},{4,3},{5,4},{6,5},{7,6},{8,7},{9,8},{10,9... | collective-permute-start | bytes 1572872 | tf_op jit(solution)/shard_map/ppermute | solution.py:19
  76.8 4.0 %collective-permute-done.6 = bf16[512,512]{1,0:T(8,128)(2,1)} collective-permute-done((bf16[512,512]{1,0:T(8,128)(2,1)S(1)}, bf16[512,512]{1,0:T(8,128)(2,1)}, u32[]{:S(2)}, u32[]{:S(2)}) %collective-permute-start.6) | collective-permute-done | bytes 524320 | tf_op jit(solution)/shard_map/ppermute | solution.py:17
  82.7 1.1 collective-permute-done.13
  83.8 3.4 %collective-permute-start.14 = (bf16[512,512]{1,0:T(8,128)(2,1)}, bf16[512,512]{1,0:T(8,128)(2,1)S(1)}, u32[]{:S(2)}, u32[]{:S(2)}) collective-permute-start(bf16[512,512]{1,0:T(8,128)(2,1)} %collective-permute-done.13), channel_id=1, source_target_pairs={{0,15},{1,0},{2,1},{3,2},{4,3},{5,4},{6,5},{7,6},{8,7},{9,8},{10,9... | collective-permute-start | bytes 1572872 | tf_op jit(solution)/shard_map/ppermute | solution.py:19
  87.2 3.7 %collective-permute-done.7 = bf16[512,512]{1,0:T(8,128)(2,1)} collective-permute-done((bf16[512,512]{1,0:T(8,128)(2,1)}, bf16[512,512]{1,0:T(8,128)(2,1)}, u32[]{:S(2)}, u32[]{:S(2)}) %collective-permute-start.7) | collective-permute-done | bytes 524320 | tf_op jit(solution)/shard_map/ppermute | solution.py:17
  90.9 1.9 %constant_dynamic-update-slice_fusion.31 = bf16[512,16384]{1,0:T(8,128)(2,1)} fusion(bf16[512,512]{1,0:T(8,128)(2,1)} %collective-permute-done.7), kind=kLoop, calls=%fused_computation.48 | loop fusion | bytes 1048576
  92.8 1.9 %constant_dynamic-update-slice_fusion.30 = bf16[512,16384]{1,0:T(8,128)(2,1)} fusion(bf16[512,16384]{1,0:T(8,128)(2,1)} %constant_dynamic-update-slice_fusion.31, bf16[512,512]{1,0:T(8,128)(2,1)} %collective-permute-done.6), kind=kLoop, calls=%fused_computation.47 | loop fusion | bytes 1048576
  94.7 1.9 %constant_dynamic-update-slice_fusion.29 = bf16[512,16384]{1,0:T(8,128)(2,1)} fusion(bf16[512,16384]{1,0:T(8,128)(2,1)} %constant_dynamic-update-slice_fusion.30, bf16[512,512]{1,0:T(8,128)(2,1)} %copy-done.13), kind=kLoop, calls=%fused_computation.46 | loop fusion | bytes 1048576
  96.6 1.9 %constant_dynamic-update-slice_fusion.28 = bf16[512,16384]{1,0:T(8,128)(2,1)} fusion(bf16[512,16384]{1,0:T(8,128)(2,1)} %constant_dynamic-update-slice_fusion.29, bf16[512,512]{1,0:T(8,128)(2,1)} %copy-done.11), kind=kLoop, calls=%fused_computation.45 | loop fusion | bytes 1048576
  98.6 1.9 %constant_dynamic-update-slice_fusion.27 = bf16[512,16384]{1,0:T(8,128)(2,1)} fusion(bf16[512,16384]{1,0:T(8,128)(2,1)} %constant_dynamic-update-slice_fusion.28, bf16[512,512]{1,0:T(8,128)(2,1)} %copy-done.9), kind=kLoop, calls=%fused_computation.44 | loop fusion | bytes 1048576
  100.5 1.9 constant_dynamic-update-slice_fusion.26
  103.2 0.9 constant_dynamic-update-slice_fusion.24
  104.1 1.9 constant_dynamic-update-slice_fusion.23
  106.8 1.9 constant_dynamic-update-slice_fusion.21
  108.7 1.9 constant_dynamic-update-slice_fusion.20
  110.5 1.9 %constant_dynamic-update-slice_fusion.19 = bf16[512,16384]{1,0:T(8,128)(2,1)} fusion(bf16[512,16384]{1,0:T(8,128)(2,1)} %constant_dynamic-update-slice_fusion.20, bf16[512,512]{1,0:T(8,128)(2,1)} %copy-done.7), kind=kLoop, calls=%fused_computation.36 | loop fusion | bytes 1048576
  112.4 1.9 constant_dynamic-update-slice_fusion.18
  114.3 1.9 constant_dynamic-update-slice_fusion.17
  117.0 1.9 %constant_dynamic-update-slice_fusion.15 = bf16[512,16384]{1,0:T(8,128)(2,1)} fusion(bf16[512,16384]{1,0:T(8,128)(2,1)} %constant_dynamic-update-slice_fusion.16, bf16[512,512]{1,0:T(8,128)(2,1)} %collective-permute-done.7), kind=kLoop, calls=%fused_computation.32 | loop fusion | bytes 1048576
  118.9 1.9 constant_dynamic-update-slice_fusion.14
  121.7 0.9 constant_dynamic-update-slice_fusion.12
  122.5 0.9 constant_dynamic-update-slice_fusion.11
  123.4 0.9 constant_dynamic-update-slice_fusion.10
  124.2 0.9 constant_dynamic-update-slice_fusion.9
  125.1 0.9 constant_dynamic-update-slice_fusion.8
  130.2 1.9 constant_dynamic-update-slice_fusion.2
  132.1 1.9 %constant_dynamic-update-slice_fusion.1 = bf16[512,16384]{1,0:T(8,128)(2,1)} fusion(bf16[512,16384]{1,0:T(8,128)(2,1)} %constant_dynamic-update-slice_fusion.2, bf16[512,512]{1,0:T(8,128)(2,1)} %collective-permute-done.13), kind=kLoop, calls=%fused_computation.18 | loop fusion | bytes 1048576
  134.0 0.9 constant_dynamic-update-slice_fusion
  134.8 9.3 %fusion = f32[512,512]{1,0:T(8,128)S(1)} fusion(bf16[8192,512]{1,0:T(8,128)(2,1)} %all-gather.2.cloned.1.call-done, bf16[512,16384]{1,0:T(8,128)(2,1)} %constant_dynamic-update-slice_fusion, s32[]{:T(128)S(6)} %select_n.14), kind=kOutput, calls=%fused_computation | convolution fusion | flops 4294967296 | bytes 17825796 | tf_op jit(solution)/shard_map/dot_general | solution.py:44
  144.3 8.6 %all-reduce.3 = (f32[128]{0:T(128)S(1)}, f32[128]{0:T(128)S(1)}, f32[128]{0:T(128)S(1)}, f32[128]{0:T(128)S(1)}) all-reduce(f32[128]{0:T(128)S(1)} %get-tuple-element.9, f32[128]{0:T(128)S(1)} %get-tuple-element.10, f32[128]{0:T(128)S(1)} %get-tuple-element.11, ...), channel_id=1, replica_groups=mesh['row_0'=4,'row_1'=4,'col'=16] {'row_0'}, use_global_device_ids=true, to_apply=%region_1.2 | all-reduce | flops 512 | bytes 4096 | tf_op jit(solution)/shard_map/psum | solution.py:26
  152.9 10.7 %all-reduce.1 = (f32[128]{0:T(128)S(1)}, f32[128]{0:T(128)S(1)}, f32[128]{0:T(128)S(1)}, f32[128]{0:T(128)S(1)}) all-reduce(f32[128]{0:T(128)S(1)} %get-tuple-element.25, f32[128]{0:T(128)S(1)} %get-tuple-element.26, f32[128]{0:T(128)S(1)} %get-tuple-element.27, ...), channel_id=1, replica_groups=mesh['row_0'=4,'row_1'=4,'col'=16] {'row_1'}, use_global_device_ids=true, to_apply=%region_2.3 | all-reduce | flops 512 | bytes 4096 | tf_op jit(solution)/shard_map/psum | solution.py:26
  163.8 10.1 %all-reduce.2 = (f32[128]{0:T(128)S(1)}, f32[128]{0:T(128)S(1)}, f32[128]{0:T(128)S(1)}, f32[128]{0:T(128)S(1)}) all-reduce(f32[128]{0:T(128)S(1)} %get-tuple-element.6, f32[128]{0:T(128)S(1)} %get-tuple-element.7, f32[128]{0:T(128)S(1)} %get-tuple-element.8, ...), channel_id=1, replica_groups=mesh['row_0'=4,'row_1'=4,'col'=16] {'row_0'}, use_global_device_ids=true, to_apply=%region_22.23 | all-reduce | flops 512 | bytes 4096 | tf_op jit(solution)/shard_map/psum | solution.py:26
  173.9 7.7 %all-reduce = (f32[128]{0:T(128)S(1)}, f32[128]{0:T(128)S(1)}, f32[128]{0:T(128)S(1)}, f32[128]{0:T(128)S(1)}) all-reduce(f32[128]{0:T(128)S(1)} %get-tuple-element.21, f32[128]{0:T(128)S(1)} %get-tuple-element.22, f32[128]{0:T(128)S(1)} %get-tuple-element.23, ...), channel_id=1, replica_groups=mesh['row_0'=4,'row_1'=4,'col'=16] {'row_1'}, use_global_device_ids=true, to_apply=%region_23.24 | all-reduce | flops 512 | bytes 4096 | tf_op jit(solution)/shard_map/psum | solution.py:26
  181.9 0.9 pad_maximum_fusion
  (66 shorter events, 13.4 us)
Async XLA Ops:
  6.5 128.3 %all-gather.2.cloned.1.call-start = ((), (), s32[]{:S(2)}) async-start(), calls=%async_computation | async-start | bytes 8912896 | tf_op jit(solution)/shard_map/all_gather | solution.py:43
  9.3 116.6 %copy-start = (bf16[512,512]{1,0:T(8,128)(2,1)S(1)}, bf16[512,512]{1,0:T(8,128)(2,1)}, u32[]{:S(2)}) copy-start(bf16[512,512]{1,0:T(8,128)(2,1)} %bitcast_multiply_fusion) | copy-start | bytes 1572868
  9.4 12.4 %collective-permute-start = (bf16[512,512]{1,0:T(8,128)(2,1)}, bf16[512,512]{1,0:T(8,128)(2,1)S(1)}, u32[]{:S(2)}, u32[]{:S(2)}) collective-permute-start(bf16[512,512]{1,0:T(8,128)(2,1)} %bitcast_multiply_fusion), channel_id=1, source_target_pairs={{0,1},{1,2},{2,3},{3,4},{4,5},{5,6},{6,7},{7,8},{8,9},{9,10},{10,1... | collective-permute-start | bytes 1572872 | tf_op jit(solution)/shard_map/ppermute | solution.py:17
  21.8 9.8 %collective-permute-start.1 = (bf16[512,512]{1,0:T(8,128)(2,1)S(1)}, bf16[512,512]{1,0:T(8,128)(2,1)S(1)}, u32[]{:S(2)}, u32[]{:S(2)}) collective-permute-start(bf16[512,512]{1,0:T(8,128)(2,1)S(1)} %collective-permute-done), channel_id=1, source_target_pairs={{0,1},{1,2},{2,3},{3,4},{4,5},{5,6},{6,7},{7,8},{8,9},{9,10},{10,1... | collective-permute-start | bytes 1572872 | tf_op jit(solution)/shard_map/ppermute | solution.py:17
  21.8 10.0 %collective-permute-start.8 = (bf16[512,512]{1,0:T(8,128)(2,1)}, bf16[512,512]{1,0:T(8,128)(2,1)S(1)}, u32[]{:S(2)}, u32[]{:S(2)}) collective-permute-start(bf16[512,512]{1,0:T(8,128)(2,1)} %bitcast_multiply_fusion), channel_id=1, source_target_pairs={{0,15},{1,0},{2,1},{3,2},{4,3},{5,4},{6,5},{7,6},{8,7},{9,8},{10,9... | collective-permute-start | bytes 1572872 | tf_op jit(solution)/shard_map/ppermute | solution.py:19
  31.6 9.8 %collective-permute-start.2 = (bf16[512,512]{1,0:T(8,128)(2,1)S(1)}, bf16[512,512]{1,0:T(8,128)(2,1)S(1)}, u32[]{:S(2)}, u32[]{:S(2)}) collective-permute-start(bf16[512,512]{1,0:T(8,128)(2,1)S(1)} %collective-permute-done.1), channel_id=1, source_target_pairs={{0,1},{1,2},{2,3},{3,4},{4,5},{5,6},{6,7},{7,8},{8,9},{9,10},{10,1... | collective-permute-start | bytes 1572872 | tf_op jit(solution)/shard_map/ppermute | solution.py:17
  31.8 10.1 %collective-permute-start.9 = (bf16[512,512]{1,0:T(8,128)(2,1)S(1)}, bf16[512,512]{1,0:T(8,128)(2,1)S(1)}, u32[]{:S(2)}, u32[]{:S(2)}) collective-permute-start(bf16[512,512]{1,0:T(8,128)(2,1)S(1)} %collective-permute-done.8), channel_id=1, source_target_pairs={{0,15},{1,0},{2,1},{3,2},{4,3},{5,4},{6,5},{7,6},{8,7},{9,8},{10,9... | collective-permute-start | bytes 1572872 | tf_op jit(solution)/shard_map/ppermute | solution.py:19
  41.4 40.3 %copy-start.3 = (bf16[512,512]{1,0:T(8,128)(2,1)}, bf16[512,512]{1,0:T(8,128)(2,1)S(1)}, u32[]{:S(2)}) copy-start(bf16[512,512]{1,0:T(8,128)(2,1)S(1)} %collective-permute-done.2) | copy-start | bytes 1572868
  41.4 9.8 %collective-permute-start.3 = (bf16[512,512]{1,0:T(8,128)(2,1)S(1)}, bf16[512,512]{1,0:T(8,128)(2,1)S(1)}, u32[]{:S(2)}, u32[]{:S(2)}) collective-permute-start(bf16[512,512]{1,0:T(8,128)(2,1)S(1)} %collective-permute-done.2), channel_id=1, source_target_pairs={{0,1},{1,2},{2,3},{3,4},{4,5},{5,6},{6,7},{7,8},{8,9},{9,10},{10,1... | collective-permute-start | bytes 1572872 | tf_op jit(solution)/shard_map/ppermute | solution.py:17
  41.9 39.8 %copy-start.1 = (bf16[512,512]{1,0:T(8,128)(2,1)}, bf16[512,512]{1,0:T(8,128)(2,1)S(1)}, u32[]{:S(2)}) copy-start(bf16[512,512]{1,0:T(8,128)(2,1)S(1)} %collective-permute-done.9) | copy-start | bytes 1572868
  41.9 9.8 %collective-permute-start.10 = (bf16[512,512]{1,0:T(8,128)(2,1)S(1)}, bf16[512,512]{1,0:T(8,128)(2,1)S(1)}, u32[]{:S(2)}, u32[]{:S(2)}) collective-permute-start(bf16[512,512]{1,0:T(8,128)(2,1)S(1)} %collective-permute-done.9), channel_id=1, source_target_pairs={{0,15},{1,0},{2,1},{3,2},{4,3},{5,4},{6,5},{7,6},{8,7},{9,8},{10,9... | collective-permute-start | bytes 1572872 | tf_op jit(solution)/shard_map/ppermute | solution.py:19
  51.2 22.1 %copy-start.9 = (bf16[512,512]{1,0:T(8,128)(2,1)}, bf16[512,512]{1,0:T(8,128)(2,1)S(1)}, u32[]{:S(2)}) copy-start(bf16[512,512]{1,0:T(8,128)(2,1)S(1)} %collective-permute-done.3) | copy-start | bytes 1572868
  51.2 9.8 %collective-permute-start.4 = (bf16[512,512]{1,0:T(8,128)(2,1)S(1)}, bf16[512,512]{1,0:T(8,128)(2,1)S(1)}, u32[]{:S(2)}, u32[]{:S(2)}) collective-permute-start(bf16[512,512]{1,0:T(8,128)(2,1)S(1)} %collective-permute-done.3), channel_id=1, source_target_pairs={{0,1},{1,2},{2,3},{3,4},{4,5},{5,6},{6,7},{7,8},{8,9},{9,10},{10,1... | collective-permute-start | bytes 1572872 | tf_op jit(solution)/shard_map/ppermute | solution.py:17
  51.7 0.8 copy-start.5
  52.5 9.8 %collective-permute-start.11 = (bf16[512,512]{1,0:T(8,128)(2,1)S(1)}, bf16[512,512]{1,0:T(8,128)(2,1)S(1)}, u32[]{:S(2)}, u32[]{:S(2)}) collective-permute-start(bf16[512,512]{1,0:T(8,128)(2,1)S(1)} %collective-permute-done.10), channel_id=1, source_target_pairs={{0,15},{1,0},{2,1},{3,2},{4,3},{5,4},{6,5},{7,6},{8,7},{9,8},{10,9... | collective-permute-start | bytes 1572872 | tf_op jit(solution)/shard_map/ppermute | solution.py:19
  61.1 15.8 %copy-start.11 = (bf16[512,512]{1,0:T(8,128)(2,1)}, bf16[512,512]{1,0:T(8,128)(2,1)S(1)}, u32[]{:S(2)}) copy-start(bf16[512,512]{1,0:T(8,128)(2,1)S(1)} %collective-permute-done.4) | copy-start | bytes 1572868
  61.1 9.8 %collective-permute-start.5 = (bf16[512,512]{1,0:T(8,128)(2,1)S(1)}, bf16[512,512]{1,0:T(8,128)(2,1)S(1)}, u32[]{:S(2)}, u32[]{:S(2)}) collective-permute-start(bf16[512,512]{1,0:T(8,128)(2,1)S(1)} %collective-permute-done.4), channel_id=1, source_target_pairs={{0,1},{1,2},{2,3},{3,4},{4,5},{5,6},{6,7},{7,8},{8,9},{9,10},{10,1... | collective-permute-start | bytes 1572872 | tf_op jit(solution)/shard_map/ppermute | solution.py:17
  62.3 0.8 copy-start.7
  63.1 10.2 %collective-permute-start.12 = (bf16[512,512]{1,0:T(8,128)(2,1)S(1)}, bf16[512,512]{1,0:T(8,128)(2,1)}, u32[]{:S(2)}, u32[]{:S(2)}) collective-permute-start(bf16[512,512]{1,0:T(8,128)(2,1)S(1)} %collective-permute-done.11), channel_id=1, source_target_pairs={{0,15},{1,0},{2,1},{3,2},{4,3},{5,4},{6,5},{7,6},{8,7},{9,8},{10,9... | collective-permute-start | bytes 1572872 | tf_op jit(solution)/shard_map/ppermute | solution.py:19
  70.9 9.9 %copy-start.13 = (bf16[512,512]{1,0:T(8,128)(2,1)}, bf16[512,512]{1,0:T(8,128)(2,1)S(1)}, u32[]{:S(2)}) copy-start(bf16[512,512]{1,0:T(8,128)(2,1)S(1)} %collective-permute-done.5) | copy-start | bytes 1572868
  70.9 9.9 %collective-permute-start.6 = (bf16[512,512]{1,0:T(8,128)(2,1)S(1)}, bf16[512,512]{1,0:T(8,128)(2,1)}, u32[]{:S(2)}, u32[]{:S(2)}) collective-permute-start(bf16[512,512]{1,0:T(8,128)(2,1)S(1)} %collective-permute-done.5), channel_id=1, source_target_pairs={{0,1},{1,2},{2,3},{3,4},{4,5},{5,6},{6,7},{7,8},{8,9},{9,10},{10,1... | collective-permute-start | bytes 1572872 | tf_op jit(solution)/shard_map/ppermute | solution.py:17
  73.3 10.5 %collective-permute-start.13 = (bf16[512,512]{1,0:T(8,128)(2,1)}, bf16[512,512]{1,0:T(8,128)(2,1)}, u32[]{:S(2)}, u32[]{:S(2)}) collective-permute-start(bf16[512,512]{1,0:T(8,128)(2,1)} %collective-permute-done.12), channel_id=1, source_target_pairs={{0,15},{1,0},{2,1},{3,2},{4,3},{5,4},{6,5},{7,6},{8,7},{9,8},{10,9... | collective-permute-start | bytes 1572872 | tf_op jit(solution)/shard_map/ppermute | solution.py:19
  80.8 10.1 %collective-permute-start.7 = (bf16[512,512]{1,0:T(8,128)(2,1)}, bf16[512,512]{1,0:T(8,128)(2,1)}, u32[]{:S(2)}, u32[]{:S(2)}) collective-permute-start(bf16[512,512]{1,0:T(8,128)(2,1)} %collective-permute-done.6), channel_id=1, source_target_pairs={{0,1},{1,2},{2,3},{3,4},{4,5},{5,6},{6,7},{7,8},{8,9},{9,10},{10,1... | collective-permute-start | bytes 1572872 | tf_op jit(solution)/shard_map/ppermute | solution.py:17
  81.8 39.0 %copy-start.14 = (bf16[512,512]{1,0:T(8,128)(2,1)S(1)}, bf16[512,512]{1,0:T(8,128)(2,1)}, u32[]{:S(2)}) copy-start(bf16[512,512]{1,0:T(8,128)(2,1)} %copy-done.13) | copy-start | bytes 1572868
  81.8 39.9 %copy-start.12 = (bf16[512,512]{1,0:T(8,128)(2,1)S(1)}, bf16[512,512]{1,0:T(8,128)(2,1)}, u32[]{:S(2)}) copy-start(bf16[512,512]{1,0:T(8,128)(2,1)} %copy-done.11) | copy-start | bytes 1572868
  81.8 40.7 %copy-start.10 = (bf16[512,512]{1,0:T(8,128)(2,1)S(1)}, bf16[512,512]{1,0:T(8,128)(2,1)}, u32[]{:S(2)}) copy-start(bf16[512,512]{1,0:T(8,128)(2,1)} %copy-done.9) | copy-start | bytes 1572868
  81.8 41.6 %copy-start.4 = (bf16[512,512]{1,0:T(8,128)(2,1)S(1)}, bf16[512,512]{1,0:T(8,128)(2,1)}, u32[]{:S(2)}) copy-start(bf16[512,512]{1,0:T(8,128)(2,1)} %copy-done.3) | copy-start | bytes 1572868
  81.8 45.8 %copy-start.2 = (bf16[512,512]{1,0:T(8,128)(2,1)S(1)}, bf16[512,512]{1,0:T(8,128)(2,1)}, u32[]{:S(2)}) copy-start(bf16[512,512]{1,0:T(8,128)(2,1)} %copy-done.1) | copy-start | bytes 1572868
  81.9 46.6 %copy-start.6 = (bf16[512,512]{1,0:T(8,128)(2,1)S(1)}, bf16[512,512]{1,0:T(8,128)(2,1)}, u32[]{:S(2)}) copy-start(bf16[512,512]{1,0:T(8,128)(2,1)} %copy-done.5) | copy-start | bytes 1572868
  81.9 47.5 %copy-start.8 = (bf16[512,512]{1,0:T(8,128)(2,1)S(1)}, bf16[512,512]{1,0:T(8,128)(2,1)}, u32[]{:S(2)}) copy-start(bf16[512,512]{1,0:T(8,128)(2,1)} %copy-done.7) | copy-start | bytes 1572868
  83.8 32.4 %collective-permute-start.14 = (bf16[512,512]{1,0:T(8,128)(2,1)}, bf16[512,512]{1,0:T(8,128)(2,1)S(1)}, u32[]{:S(2)}, u32[]{:S(2)}) collective-permute-start(bf16[512,512]{1,0:T(8,128)(2,1)} %collective-permute-done.13), channel_id=1, source_target_pairs={{0,15},{1,0},{2,1},{3,2},{4,3},{5,4},{6,5},{7,6},{8,7},{9,8},{10,9... | collective-permute-start | bytes 1572872 | tf_op jit(solution)/shard_map/ppermute | solution.py:19
Sparse Core Ops, SparseCore 0:
  9.8 78.7 all-gather.1
